TPU v7x, 32 devices: a whole 2x2x4 slice. The times are simulated.
32 devices in a mesh: year: 8 (over y, x, core), port: 4 (over z).
Axes of the slice: x: 2, y: 2, z: 4, core: 2. Of those that a mesh axis runs over, the one named last changes fastest.
Arguments:
- event_loss: bfloat16 [4096, 4096], P('year', 'port'), may hold values from 0 to 24
- event_year: int32 [4096], P('year'), may hold values from -1 to 255, as said below
- retention: float32 [4096], P('port'), may hold values from 0.2 to 2
- risk_limit: float32 [4096], P('port'), may hold values from 1 to 8
- cession_share: bfloat16 [4096, 4], P('port'), may hold values from 0.099609375 to 1
- member_treaty: int32 [4096, 4], P('port'), may hold values from 0 to 1023, all different within a row
- attach_tier: int32 [1024], P('port'), may hold values from 2 to 11
- limit_tier: int32 [1024], P('port'), may hold values from 2 to 10
- reinstatements: int32 [1024], P('port'), may hold values from 0 to 3
- reinstate_rate: float32 [1024], P('port'), may hold values from 0.1 to 1
- stop_attach: float32 [1024], P('port'), may hold values from 0.7 to 2
- stop_width: float32 [1024], P('port'), may hold values from 0.3 to 2
Outputs:
- layer_net: float32 [1024, 256], P('port', 'year')
- stop_loss: float32 [1024, 256], P('port', 'year')
- tail_mean: float32 [1024], P('port')
Inputs may be any that keep to these rules, and one draw needn't show every extreme that they name: `event_year`: the 512 rows of year-block b name years b * 32 to (b + 1) * 32 - 1 in nondecreasing order, followed by padding rows marked -1; at least one block has no padding row. `member_treaty`: each portfolio names 4 different treaties, and every treaty is named by some portfolio.
All inputs are finite; a program needn't handle non-finite values.
Results may differ from a plain program's by a relative error of at most 0.029.
Values may be sent and summed in bfloat16 or wider, within the bound.
A program may use at most 64 MiB of HBM per device.

v0:
```python
import jax
import jax.numpy as jnp
from jax import lax
from jax.sharding import PartitionSpec as P

TREATIES = 1024
MEMB = 4
YEAR_DEV = 32
TAIL = 16


UNIT_LOSS = 1.0


def combined_all(part, axis, combine):
    gathered = lax.all_gather(part, axis)

    def take(source):
        return lax.dynamic_index_in_dim(gathered, source, 0, False)

    return lax.fori_loop(
        1, lax.axis_size(axis), lambda source, state: combine(state, take(source)), take(0)
    )


def clamp_between(values, lower, upper):
    return jnp.minimum(jnp.maximum(values, lower), upper)


def top_years(values, keep_count):
    return jnp.sort(values, axis=1)[:, values.shape[1] - keep_count :]


def on_device(
    event_loss,
    event_year,
    retention,
    risk_limit,
    cession_share,
    member_treaty,
    attach_tier,
    limit_tier,
    reinstatements,
    reinstate_rate,
    stop_attach,
    stop_width,
):
    own_count = attach_tier.shape[0]
    ceded_loss = clamp_between(
        event_loss.astype(jnp.float32) - retention[None, :], 0.0, risk_limit[None, :]
    ).astype(jnp.bfloat16)
    treaty_ids = lax.broadcasted_iota(jnp.int32, (1, TREATIES), 1)
    weights = jnp.zeros((event_loss.shape[1], TREATIES), jnp.float32)
    for member_slot in range(MEMB):
        picked = member_treaty[:, member_slot : member_slot + 1] == treaty_ids
        weights = weights + jnp.where(
            picked, cession_share[:, member_slot : member_slot + 1].astype(jnp.float32), 0.0
        )
    weights = weights.astype(jnp.bfloat16)
    first_year = lax.axis_index("year") * YEAR_DEV
    local_year = event_year - first_year
    contract = (((0,), (1,)), ((), ()))
    event_treaty = lax.psum_scatter(
        lax.dot_general(weights, ceded_loss, contract, preferred_element_type=jnp.float32).astype(
            jnp.bfloat16
        ),
        "port",
        scatter_dimension=0,
        tiled=True,
    ).astype(jnp.float32)
    attach = attach_tier.astype(jnp.float32) * UNIT_LOSS
    limit_loss = limit_tier.astype(jnp.float32) * UNIT_LOSS
    recovered = clamp_between(event_treaty - attach[:, None], 0.0, limit_loss[:, None])
    retained = event_treaty - recovered
    year_hits = (local_year[:, None] == lax.broadcasted_iota(jnp.int32, (1, YEAR_DEV), 1)).astype(
        jnp.float32
    )
    yearly = jnp.dot(
        jnp.concatenate((recovered, retained), 0),
        year_hits,
        precision=lax.Precision.HIGHEST,
        preferred_element_type=jnp.float32,
    )
    annual = yearly[:own_count]
    kept_annual = yearly[own_count:]
    reinstated = reinstatements.astype(jnp.float32)
    layer_paid = jnp.minimum(annual, ((1.0 + reinstated) * limit_loss)[:, None])
    layer_net = (
        layer_paid
        - reinstate_rate[:, None] * jnp.minimum(layer_paid, (reinstated * limit_loss)[:, None])
    ) / limit_loss[:, None]
    year_total = YEAR_DEV * lax.axis_size("year")
    summed = lax.psum(jnp.sum(kept_annual, axis=1), "year")
    base_loss = UNIT_LOSS + summed / year_total
    loss_ratio = kept_annual / base_loss[:, None]

    def keep_largest(earlier, later):
        return top_years(jnp.concatenate((earlier, later), 1), TAIL)

    largest = combined_all(top_years(loss_ratio, TAIL), "year", keep_largest)
    tail_mean = jnp.mean(largest, axis=1)
    stop_loss = clamp_between(loss_ratio - stop_attach[:, None], 0.0, stop_width[:, None])
    return (layer_net, stop_loss, tail_mean)


def solution(mesh):
    return jax.shard_map(
        on_device,
        mesh=mesh,
        in_specs=(
            P("year", "port"),
            P("year"),
            P("port"),
            P("port"),
            P("port", None),
            P("port", None),
            P("port"),
            P("port"),
            P("port"),
            P("port"),
            P("port"),
            P("port"),
        ),
        out_specs=(P("port", "year"), P("port", "year"), P("port")),
        check_vma=False,
    )
```

profile of v0, /device:TPU:0, one launch (start us, length us, event | category | flops | bytes accessed | tf_op | source)
XLA Modules:
  0.0 85.3 jit_solution(53839467080890265)
XLA Ops:
  7.2 0.0 reduce-scatter.2.cloned.1.call-start
  7.2 0.9 %fusion.23 = (s32[1024,1]{0,1:T(1,128)S(1)}, s32[1024,1]{0,1:T(1,128)S(1)}, s32[1024,1]{0,1:T(1,128)S(1)}, s32[1024,1]{0,1:T(1,128)S(1)}) fusion(s32[1024,4]{0,1:T(4,128)} %param.19), kind=kLoop, calls=%fused_computation.49 | loop fusion | bytes 32768 | tf_op jit(solution)/shard_map/slice | solution.py:55
  8.1 0.9 %slice_convert_fusion.3 = (f32[1024,1]{0,1:T(1,128)S(1)}, f32[1024,1]{0,1:T(1,128)S(1)}, f32[1024,1]{0,1:T(1,128)S(1)}, f32[1024,1]{0,1:T(1,128)S(1)}) fusion(bf16[1024,4]{0,1:T(4,128)(2,1)} %param.18), kind=kLoop, calls=%fused_computation.41 | loop fusion | flops 4096 | bytes 24576 | tf_op jit(solution)/shard_map/jit(_where)/broadcast_in_dim | solution.py:56
  9.0 5.4 %fusion.10 = bf16[1024,512]{1,0:T(8,128)(2,1)} fusion(f32[1024]{0:T(1024)S(1)} %bitcast.26, s32[1024]{0:T(1024)S(1)} %bitcast.22, f32[1024]{0:T(1024)S(1)} %bitcast.27, s32[1024]{0:T(1024)S(1)} %bitcast.23, f32[1024]{0:T(1024)S(1)} %bitcast.25, s32[1024]{0:T(1024)S(1)} %bitcast.21, f32[1024]{0:T(1024)S(1)} %bitcast.24, s32[1024]{0:T(1024)S(1)} %bitcast.20, ...), kind=kOutput, calls=%fused_computation.19 | convolution fusion | flops 1089994752 | bytes 2138112 | tf_op jit(solution)/shard_map/dot_general | solution.py:64
  14.4 0.0 copy-start
  14.4 0.0 copy-start.5
  14.4 0.0 copy-start.6
  14.4 0.0 copy-start.1
  14.4 0.0 reduce-scatter.2.cloned.1.call-update
  14.5 0.6 copy-done
  15.1 0.0 copy-done.5
  15.1 0.0 copy-done.6
  15.1 0.0 copy-done.1
  15.1 0.0 copy-start.2
  15.2 0.0 copy-start.3
  15.2 0.0 copy-start.4
  15.2 29.4 %reduce-scatter.2.cloned.1.call-done = bf16[256,512]{1,0:T(8,128)(2,1)} async-done(((bf16[1024,512]{1,0:T(8,128)(2,1)}), bf16[256,512]{1,0:T(8,128)(2,1)}) %reduce-scatter.2.cloned.1.call-update) | async-done | bytes 262160 | tf_op jit(solution)/shard_map/reduce_scatter | solution.py:63
  44.6 1.1 %fusion.19 = (f32[256,512]{1,0:T(8,128)S(1)}, f32[256,512]{1,0:T(8,128)S(1)}) fusion(bf16[256,512]{1,0:T(8,128)(2,1)} %reduce-scatter.2.cloned.1.call-done, f32[256]{0:T(256)S(1)} %convert_element_type.35, f32[256]{0:T(256)S(1)} %convert_element_type.34), kind=kLoop, calls=%fused_computation.30 | loop fusion | flops 655360 | bytes 1312768 | tf_op jit(solution)/shard_map/min | solution.py:27
  45.8 0.7 fusion.11
  46.5 13.2 %psum.7 = f32[256]{0:T(256)S(1)} all-reduce(f32[256]{0:T(256)S(1)} %slice_reduce_fusion), channel_id=1, replica_groups=mesh['year'=8,'port'=4] {'year'}, use_global_device_ids=true, to_apply=%region_2.3 | all-reduce | flops 256 | bytes 2048 | tf_op jit(solution)/shard_map/psum | solution.py:93
  59.7 0.0 copy-done.2
  59.7 0.0 copy-done.3
  59.7 0.0 copy-done.4
  59.7 0.6 maximum_minimum_fusion
  60.4 1.1 %sort.34 = (f32[256,32]{0,1:T(8,128)S(1)}, s32[256,32]{0,1:T(8,128)}) sort(f32[256,32]{0,1:T(8,128)S(1)} %get-tuple-element.107, s32[256,32]{0,1:T(8,128)S(1)} %iota.16), dimensions={1}, to_apply=%region_3.4 | sort | flops 106496 | bytes 131072 | tf_op jit(solution)/shard_map/jit(sort)/sort | solution.py:31
  61.5 8.3 %all-gather = f32[2048,16]{0,1:T(8,128)S(1)} all-gather(f32[256,16]{0,1:T(8,128)S(1)} %slice.54), channel_id=2, replica_groups=mesh['year'=8,'port'=4] {'year'}, dimensions={0}, use_global_device_ids=true | all-gather | bytes 147456 | tf_op jit(solution)/shard_map/all_gather | solution.py:16
  69.8 8.1 %while.15 = (s32[]{:T(128)}, f32[256,16]{0,1:T(8,128)S(1)}, f32[8,256,16]{1,0,2:T(8,128)S(1)}, s32[]{:T(128)}, s32[]{:T(128)}, /*index=5*/s32[]{:T(128)}) while((s32[]{:T(128)}, f32[256,16]{0,1:T(8,128)S(1)}, f32[8,256,16]{1,0,2:T(8,128)S(1)}, s32[]{:T(128)}, s32[]{:T(128)}, /*index=5*/s32[]{:T(128)}) %tuple.56), condition=%wide.region_6.7_spmd, body=%wide.region_4.6_spmd.sunk | while | flops 114693 | bytes 327795 | solution.py:21
  69.9 1.1 %sort.36 = (f32[256,32]{0,1:T(8,128)S(1)}, s32[256,32]{0,1:T(8,128)}) sort(f32[256,32]{0,1:T(8,128)S(1)} %pad_maximum_fusion.2, s32[256,32]{0,1:T(8,128)S(1)} %iota.18), dimensions={1}, to_apply=%region_5.5 | sort | flops 106496 | bytes 131072 | tf_op jit(solution)/shard_map/while/body/eval_jaxpr/jit(sort)/sort | solution.py:31
  71.0 1.1 %sort.36 = (f32[256,32]{0,1:T(8,128)S(1)}, s32[256,32]{0,1:T(8,128)}) sort(f32[256,32]{0,1:T(8,128)S(1)} %pad_maximum_fusion.2, s32[256,32]{0,1:T(8,128)S(1)} %iota.18), dimensions={1}, to_apply=%region_5.5 | sort | flops 106496 | bytes 131072 | tf_op jit(solution)/shard_map/while/body/eval_jaxpr/jit(sort)/sort | solution.py:31
  72.2 1.1 %sort.36 = (f32[256,32]{0,1:T(8,128)S(1)}, s32[256,32]{0,1:T(8,128)}) sort(f32[256,32]{0,1:T(8,128)S(1)} %pad_maximum_fusion.2, s32[256,32]{0,1:T(8,128)S(1)} %iota.18), dimensions={1}, to_apply=%region_5.5 | sort | flops 106496 | bytes 131072 | tf_op jit(solution)/shard_map/while/body/eval_jaxpr/jit(sort)/sort | solution.py:31
  73.3 1.1 %sort.36 = (f32[256,32]{0,1:T(8,128)S(1)}, s32[256,32]{0,1:T(8,128)}) sort(f32[256,32]{0,1:T(8,128)S(1)} %pad_maximum_fusion.2, s32[256,32]{0,1:T(8,128)S(1)} %iota.18), dimensions={1}, to_apply=%region_5.5 | sort | flops 106496 | bytes 131072 | tf_op jit(solution)/shard_map/while/body/eval_jaxpr/jit(sort)/sort | solution.py:31
  74.5 1.1 %sort.36 = (f32[256,32]{0,1:T(8,128)S(1)}, s32[256,32]{0,1:T(8,128)}) sort(f32[256,32]{0,1:T(8,128)S(1)} %pad_maximum_fusion.2, s32[256,32]{0,1:T(8,128)S(1)} %iota.18), dimensions={1}, to_apply=%region_5.5 | sort | flops 106496 | bytes 131072 | tf_op jit(solution)/shard_map/while/body/eval_jaxpr/jit(sort)/sort | solution.py:31
  75.6 1.1 %sort.36 = (f32[256,32]{0,1:T(8,128)S(1)}, s32[256,32]{0,1:T(8,128)}) sort(f32[256,32]{0,1:T(8,128)S(1)} %pad_maximum_fusion.2, s32[256,32]{0,1:T(8,128)S(1)} %iota.18), dimensions={1}, to_apply=%region_5.5 | sort | flops 106496 | bytes 131072 | tf_op jit(solution)/shard_map/while/body/eval_jaxpr/jit(sort)/sort | solution.py:31
  76.8 1.1 %sort.36 = (f32[256,32]{0,1:T(8,128)S(1)}, s32[256,32]{0,1:T(8,128)}) sort(f32[256,32]{0,1:T(8,128)S(1)} %pad_maximum_fusion.2, s32[256,32]{0,1:T(8,128)S(1)} %iota.18), dimensions={1}, to_apply=%region_5.5 | sort | flops 106496 | bytes 131072 | tf_op jit(solution)/shard_map/while/body/eval_jaxpr/jit(sort)/sort | solution.py:31
  77.9 0.6 broadcast_multiply_fusion
  (46 shorter events, 0.3 us)
Async XLA Ops:
  7.2 37.4 %reduce-scatter.2.cloned.1.call-start = ((), (), s32[]{:S(2)}) async-start(), calls=%async_computation.1 | async-start | bytes 1310720 | tf_op jit(solution)/shard_map/reduce_scatter | solution.py:63
  14.4 0.7 copy-start
  14.4 0.7 copy-start.5
  14.4 0.7 copy-start.6
  14.4 0.7 copy-start.1
  15.1 44.5 %copy-start.2 = (f32[256]{0:T(256)S(1)}, f32[256]{0:T(256)}, u32[]{:S(2)}) copy-start(f32[256]{0:T(256)} %param.25) | copy-start | bytes 3076
  15.2 44.5 %copy-start.3 = (f32[256]{0:T(256)S(1)}, f32[256]{0:T(256)}, u32[]{:S(2)}) copy-start(f32[256]{0:T(256)} %param.24) | copy-start | bytes 3076
  15.2 44.5 %copy-start.4 = (f32[256]{0:T(256)S(1)}, f32[256]{0:T(256)}, u32[]{:S(2)}) copy-start(f32[256]{0:T(256)} %param.23) | copy-start | bytes 3076
Sparse Core Ops, SparseCore 0:
  14.6 29.9 reduce-scatter.1
where the time goes:
time: 85.7 us; the launch traced here: 85.3 us
  waiting for transfers between devices  29.4 us (34%)
  blocking collectives  21.5 us (25%)
  between operations  14.1 us (16%)
  other arithmetic  12.1 us (14%)
  matrix products  6.14 us (7%)
  local copies, waits for them, and re-layouts  1.82 us (2%)
    reduce_scatter x1, waiting for transfers between devices, on_device(): lax.psum_scatter(lax.dot_general(weights, ceded_loss, contract, preferred...  29.4 us
    psum x1, blocking collectives, on_device(): summed = lax.psum(jnp.sum(kept_annual, axis=1), 'year')  13.2 us
    sort x8, other arithmetic, top_years(): return jnp.sort(values, axis=1)[:, values.shape[1] - keep_count:]  8.77 us
    all_gather x1, blocking collectives, combined_all(): gathered = lax.all_gather(part, axis)  8.27 us
    dot_general x1, matrix products, on_device(): lax.dot_general(weights, ceded_loss, contract, preferred_element_type=jnp...  5.45 us
    min x2, other arithmetic, clamp_between(): return jnp.minimum(jnp.maximum(values, lower), upper)  1.78 us
  transfers between devices with their start and end apart: 1, of which 1 were waited for; matrix products, arithmetic and copies ran while one was open for 0% of the time, Pallas kernels for 0%

commit v1 on v0

v1 whole, which is shorter than its diff:
```python
import functools

import jax
import jax.numpy as jnp
from jax import lax
from jax.experimental import pallas as pl
from jax.experimental.pallas import tpu as pltpu
from jax.sharding import PartitionSpec as P

TREATIES = 1024
YEAR_DEV = 32
TAIL = 16
LANES = 128
SUBLANES = 8
UNIT_LOSS = 1.0
MESH = pl.DeviceIdType.MESH


def clamp_between(values, lower, upper):
    return jnp.minimum(jnp.maximum(values, lower), upper)


def exchange(items, low, high):
    larger = jnp.maximum(items[low], items[high])
    items[high] = jnp.minimum(items[low], items[high])
    items[low] = larger


def sort_network(count):
    pairs = []
    width = 1
    while width < count:
        step = width
        while step >= 1:
            for start in range(step % width, count - step, 2 * step):
                for offset in range(min(step, count - start - step)):
                    low = start + offset
                    if low // (2 * width) == (low + step) // (2 * width):
                        pairs.append((low, low + step))
            step //= 2
        width *= 2
    return pairs


def sort_falling(items):
    items = list(items)
    for low, high in sort_network(len(items)):
        exchange(items, low, high)
    return items


def merge_largest(first, second, ordered):
    count = len(first)
    items = [jnp.maximum(first[i], second[count - 1 - i]) for i in range(count)]
    step = count // 2
    while ordered and step >= 1:
        for low in range(count):
            if low & step == 0:
                exchange(items, low, low + step)
        step //= 2
    return items


def largest_sum(values):
    rows = values.shape[0]
    tiles = [values[start : start + SUBLANES] for start in range(0, rows, SUBLANES)]
    runs = [sort_falling(tiles[start : start + TAIL]) for start in range(0, len(tiles), TAIL)]
    while len(runs) > 1:
        merged = [
            merge_largest(runs[i], runs[i + 1], True) for i in range(0, len(runs) - 1, 2)
        ]
        runs = merged + runs[len(merged) * 2 :]
    best = runs[0]
    shift = SUBLANES // 2
    while shift >= 1:
        rolled = [pltpu.roll(item, shift, 0) for item in best]
        best = merge_largest(best, rolled, shift > 1)
        shift //= 2
    total = best[0]
    for item in best[1:]:
        total = total + item
    return total[0:1]


def kernel(
    sizes,
    loss_ref,
    year_ref,
    retention_ref,
    risk_ref,
    share_ref,
    member_ref,
    attach_ref,
    limit_ref,
    reinst_ref,
    rate_ref,
    stop_attach_ref,
    stop_width_ref,
    net_ref,
    stop_ref,
    tail_ref,
    ceded,
    sending,
    landing,
    held,
    own_sum,
    kept,
    port_send,
    port_recv,
    year_send,
    year_recv,
):
    n_year, n_port, own, groups = sizes
    rows, ports = loss_ref.shape
    me_port = lax.axis_index("port")
    me_year = lax.axis_index("year")

    barrier = pltpu.get_barrier_semaphore()
    for step in range(1, n_port):
        peer = lax.rem(me_port + step, n_port)
        pl.semaphore_signal(barrier, inc=1, device_id={"port": peer}, device_id_type=MESH)
    for step in range(1, n_year):
        peer = lax.rem(me_year + step, n_year)
        pl.semaphore_signal(barrier, inc=1, device_id={"year": peer}, device_id_type=MESH)

    ceded[...] = clamp_between(
        loss_ref[...].astype(jnp.float32) - retention_ref[...], 0.0, risk_ref[...]
    ).astype(jnp.bfloat16)

    def product(dest, group):
        lane = lax.broadcasted_iota(jnp.int32, (LANES, ports), 0) + group * LANES
        treaty = lane + dest * own
        if own % LANES:
            treaty = jnp.where(lane < own, treaty, -1)
        weights = jnp.zeros((LANES, ports), jnp.float32)
        for slot in range(member_ref.shape[0]):
            weights = jnp.where(
                member_ref[slot : slot + 1, :] == treaty,
                share_ref[slot : slot + 1, :].astype(jnp.float32),
                weights,
            )
        return lax.dot_general(
            ceded[...],
            weights.astype(jnp.bfloat16),
            (((1,), (1,)), ((), ())),
            preferred_element_type=jnp.float32,
        )

    def port_copy(piece, group, device, slot):
        return pltpu.make_async_remote_copy(
            src_ref=sending.at[piece, group],
            dst_ref=landing.at[slot, group],
            send_sem=port_send.at[piece, group],
            recv_sem=port_recv.at[slot, group],
            device_id={"port": device},
            device_id_type=MESH,
        )

    def wait_landed(slot, group):
        port_copy(0, group, me_port, slot).wait_recv()

    waited = []

    def entered():
        if not waited:
            pl.semaphore_wait(barrier, n_port + n_year - 2)
            waited.append(True)

    copies = []
    if n_port == 4:
        is_end = (me_port == 0) | (me_port == 3)
        near = me_port + 1 - 2 * lax.rem(me_port, 2)
        low_half = me_port < 2
        far_end = jnp.where(low_half, 3, 0)
        far_middle = jnp.where(low_half, 2, 1)
        for group in range(groups):
            dest = jnp.where(is_end, far_middle, far_end)
            sending[0, group] = product(dest, group).astype(jnp.bfloat16)
            entered()
            copy = port_copy(0, group, jnp.where(is_end, near, far_end), 2)
            copy.start()
            copies.append(copy)

            dest = jnp.where(is_end, far_end, near)
            sending[1, group] = product(dest, group).astype(jnp.bfloat16)
            copy = port_copy(1, group, dest, jnp.where(is_end, 1, 0))
            copy.start()
            copies.append(copy)

            last = product(jnp.where(is_end, near, far_middle), group)
            held[group] = last
            copy = port_copy(
                2, group, jnp.where(is_end, near, far_middle), jnp.where(is_end, 0, 1)
            )
            copies.append(copy)

            @pl.when(is_end)
            def _():
                sending[2, group] = held[group].astype(jnp.bfloat16)
                copy.start()

        for group in range(groups):
            own_sum[group] = product(me_port, group)
        for group in range(groups):
            copy = copies[3 * group + 2]

            @pl.when(jnp.logical_not(is_end))
            def _():
                wait_landed(2, group)
                sending[2, group] = (
                    held[group] + landing[2, group].astype(jnp.float32)
                ).astype(jnp.bfloat16)
                copy.start()

    else:
        for group in range(groups):
            for step in range(1, n_port):
                dest = lax.rem(me_port + step, n_port)
                sending[step - 1, group] = product(dest, group).astype(jnp.bfloat16)
                entered()
                copy = port_copy(step - 1, group, dest, step - 1)
                copy.start()
                copies.append(copy)
        for group in range(groups):
            own_sum[group] = product(me_port, group)
    entered()

    local_year = year_ref[...] - me_year * YEAR_DEV
    hits = (
        (local_year == lax.broadcasted_iota(jnp.int32, (YEAR_DEV, rows), 0))
        .astype(jnp.float32)
        .astype(jnp.bfloat16)
    )

    def split_dot(values):
        upper = values.astype(jnp.bfloat16)
        lower = (values - upper.astype(jnp.float32)).astype(jnp.bfloat16)
        return jnp.dot(hits, upper, preferred_element_type=jnp.float32) + jnp.dot(
            hits, lower, preferred_element_type=jnp.float32
        )

    def year_copy(step, group):
        return pltpu.make_async_remote_copy(
            src_ref=kept.at[group, me_year],
            dst_ref=kept.at[group, me_year],
            send_sem=year_send.at[group, step - 1],
            recv_sem=year_recv.at[group, me_year],
            device_id={"year": lax.rem(me_year + step, n_year)},
            device_id_type=MESH,
        )

    for group in range(groups):
        lanes = slice(group * LANES, (group + 1) * LANES)
        event_treaty = own_sum[group]
        if n_port == 4:
            wait_landed(0, group)
            wait_landed(1, group)

            @pl.when(is_end)
            def _():
                wait_landed(2, group)

            event_treaty = event_treaty + landing[0, group].astype(jnp.float32)
            event_treaty = event_treaty + landing[1, group].astype(jnp.float32)
            event_treaty = event_treaty + jnp.where(
                is_end, landing[2, group].astype(jnp.float32), 0.0
            )
        else:
            for slot in range(n_port - 1):
                wait_landed(slot, group)
                event_treaty = event_treaty + landing[slot, group].astype(jnp.float32)
        attach = attach_ref[:, lanes].astype(jnp.float32) * UNIT_LOSS
        limit_loss = limit_ref[:, lanes].astype(jnp.float32) * UNIT_LOSS
        recovered = clamp_between(event_treaty - attach, 0.0, limit_loss)
        retained = event_treaty - recovered
        yearly = split_dot(jnp.concatenate((recovered, retained), 1))
        annual = yearly[:, :LANES]
        kept[group, me_year] = yearly[:, LANES:]
        for step in range(1, n_year):
            copy = year_copy(step, group)
            copy.start()
            copies.append(copy)
        reinstated = reinst_ref[:, lanes].astype(jnp.float32)
        layer_paid = jnp.minimum(annual, (1.0 + reinstated) * limit_loss)
        net_ref[:, lanes] = (
            layer_paid
            - rate_ref[:, lanes] * jnp.minimum(layer_paid, reinstated * limit_loss)
        ) / limit_loss

    for group in range(groups):
        lanes = slice(group * LANES, (group + 1) * LANES)
        for step in range(1, n_year):
            source = lax.rem(me_year + step, n_year)
            pltpu.make_async_remote_copy(
                src_ref=kept.at[group, source],
                dst_ref=kept.at[group, source],
                send_sem=year_send.at[group, step - 1],
                recv_sem=year_recv.at[group, source],
                device_id={"year": source},
                device_id_type=MESH,
            ).wait_recv()
        every = kept[group].reshape(n_year * YEAR_DEV, LANES)
        base_loss = UNIT_LOSS + jnp.sum(every, axis=0, keepdims=True) / (n_year * YEAR_DEV)
        tail_ref[:, lanes] = largest_sum(every) / base_loss / TAIL
        loss_ratio = kept[group, me_year] / base_loss
        stop_ref[:, lanes] = clamp_between(
            loss_ratio - stop_attach_ref[:, lanes], 0.0, stop_width_ref[:, lanes]
        )

    for copy in copies:
        copy.wait_send()


def on_device(sizes, event_loss, event_year, retention, risk_limit, share, member, *terms):
    n_year, n_port, own, groups = sizes
    rows, ports = event_loss.shape
    padded = groups * LANES

    def row(values):
        return values.reshape(1, values.shape[0])

    def term_row(values):
        if padded != own:
            values = jnp.pad(values, (0, padded - own), constant_values=1)
        return row(values)

    vmem = pl.BlockSpec(memory_space=pltpu.VMEM)
    pieces = n_port - 1
    layer_net, stop_loss, tail_mean = pl.pallas_call(
        functools.partial(kernel, sizes),
        name="layers",
        out_shape=(
            jax.ShapeDtypeStruct((YEAR_DEV, padded), jnp.float32),
            jax.ShapeDtypeStruct((YEAR_DEV, padded), jnp.float32),
            jax.ShapeDtypeStruct((1, padded), jnp.float32),
        ),
        in_specs=[vmem] * 12,
        out_specs=(vmem, vmem, vmem),
        scratch_shapes=[
            pltpu.VMEM((rows, ports), jnp.bfloat16),
            pltpu.VMEM((pieces, groups, rows, LANES), jnp.bfloat16),
            pltpu.VMEM((pieces, groups, rows, LANES), jnp.bfloat16),
            pltpu.VMEM((groups, rows, LANES), jnp.float32),
            pltpu.VMEM((groups, rows, LANES), jnp.float32),
            pltpu.VMEM((groups, n_year, YEAR_DEV, LANES), jnp.float32),
            pltpu.SemaphoreType.DMA((pieces, groups)),
            pltpu.SemaphoreType.DMA((pieces, groups)),
            pltpu.SemaphoreType.DMA((groups, n_year)),
            pltpu.SemaphoreType.DMA((groups, n_year)),
        ],
        compiler_params=pltpu.CompilerParams(collective_id=0, has_side_effects=True),
    )(
        event_loss,
        row(event_year),
        row(retention),
        row(risk_limit),
        share.T,
        member.T,
        *[term_row(values) for values in terms],
    )
    return layer_net[:, :own].T, stop_loss[:, :own].T, tail_mean[0, :own]


def solution(mesh):
    n_year, n_port = mesh.shape["year"], mesh.shape["port"]
    own = TREATIES // n_port
    groups = -(-own // LANES)
    return jax.shard_map(
        functools.partial(on_device, (n_year, n_port, own, groups)),
        mesh=mesh,
        in_specs=(
            P("year", "port"),
            P("year"),
            P("port"),
            P("port"),
            P("port", None),
            P("port", None),
            P("port"),
            P("port"),
            P("port"),
            P("port"),
            P("port"),
            P("port"),
        ),
        out_specs=(P("port", "year"), P("port", "year"), P("port")),
        check_vma=False,
    )
```

time: 85.7 us -> 33.4 us (0.39)
  Pallas kernels: 0 us -> 29.9 us
  waiting for transfers between devices: 29.4 us -> 0 us
  blocking collectives: 21.5 us -> 0 us
  between operations: 14.1 us -> 0.65 us
  other arithmetic: 12.1 us -> 0 us
  matrix products: 6.14 us -> 0 us
    pallas_call x0 -> x1, Pallas kernels: none -> 29.9 us  [on_device(): pl.pallas_call(functools.partial(kernel, sizes), name='layers', out_shape...]
    reduce_scatter x1 -> x0, waiting for transfers between devices: 29.4 us -> none  [on_device(): lax.psum_scatter(lax.dot_general(weights, ceded_loss, contract, preferred...]
    psum x1 -> x0, blocking collectives: 13.2 us -> none  [on_device(): summed = lax.psum(jnp.sum(kept_annual, axis=1), 'year')]
    sort x8 -> x0, other arithmetic: 8.77 us -> none  [top_years(): return jnp.sort(values, axis=1)[:, values.shape[1] - keep_count:]]
    all_gather x1 -> x0, blocking collectives: 8.27 us -> none  [combined_all(): gathered = lax.all_gather(part, axis)]
    dot_general x2 -> x0, matrix products: 6.14 us -> none  [the longest x1 5.45 us: on_device(): lax.dot_general(weights, ceded_loss, contract, preferred_element_type=jnp...]
    unnamed x15 -> x7, local copies, waits for them, and re-layouts: 0.74 us -> 2.63 us
    min x2 -> x0, other arithmetic: 1.78 us -> none  [clamp_between(): return jnp.minimum(jnp.maximum(values, lower), upper)]
  transfers between devices with their start and end apart: 1 -> 0, of which waited for: 1 -> 0; matrix products, arithmetic and copies ran while one was open for 0% -> 0% of each run, Pallas kernels for 0% -> 0%
where the time goes in v1:
time: 33.4 us; the launch traced here: 33.2 us
  Pallas kernels  29.9 us (90%)
  local copies, waits for them, and re-layouts  2.63 us (8%)
  between operations  0.65 us (2%)
    pallas_call x1, Pallas kernels, on_device(): pl.pallas_call(functools.partial(kernel, sizes), name='layers', out_shape...  29.9 us
    unnamed x7, local copies, waits for them, and re-layouts  2.63 us

profile of v1, /device:TPU:0, one launch (start us, length us, event | category | flops | bytes accessed | tf_op | source)
XLA Modules:
  0.0 33.2 jit_solution(3480132113386298467)
XLA Ops:
  0.6 29.9 %layers.1 = (f32[32,256]{1,0:T(8,128)}, f32[32,256]{1,0:T(8,128)}, f32[1,256]{1,0:T(1,128)}) custom-call(bf16[512,1024]{1,0:T(8,128)(2,1)} %loss_ref.1, s32[1,512]{1,0:T(1,128)} %bitcast.20, f32[1,1024]{1,0:T(1,128)} %bitcast.18, f32[1,1024]{1,0:T(1,128)} %bitcast.19, bf16[4,1024]{1,0:T(4,128)(2,1)} %bitcast.17, s32[4,1024]{1,0:T(4,128)} %bitcast.16, ...), custom_call_target="tpu_custom_call" | custom-call | tf_op jit(solution)/shard_map/layers/pallas_call | solution.py:329
  30.6 0.0 copy-start
  30.6 1.4 %copy.18 = f32[256,32]{0,1:T(8,128)} copy(f32[256,32]{0,1:T(8,128)} %bitcast.15) | data formatting | bytes 65536
  31.9 0.0 copy-done
  31.9 0.0 copy-start.1
  31.9 0.6 %copy.19 = f32[256,32]{0,1:T(8,128)} copy(f32[256,32]{0,1:T(8,128)S(1)} %bitcast.14) | data formatting | bytes 65536
  32.6 0.1 copy-done.1
  32.6 0.6 %copy.20 = f32[256]{0:T(256)} copy(f32[256]{0:T(256)S(1)} %bitcast.21) | data formatting | bytes 2048
Async XLA Ops:
  30.6 1.4 %copy-start = (f32[32,256]{1,0:T(8,128)S(1)}, f32[32,256]{1,0:T(8,128)}, u32[]{:S(2)}) copy-start(f32[32,256]{1,0:T(8,128)} %get-tuple-element.7) | copy-start | bytes 98308
  31.9 0.7 %copy-start.1 = (f32[1,256]{1,0:T(1,128)S(1)}, f32[1,256]{1,0:T(1,128)}, u32[]{:S(2)}) copy-start(f32[1,256]{1,0:T(1,128)} %get-tuple-element.8) | copy-start | bytes 3076

commit v2 on v1

--- a/solution.py
+++ b/solution.py
@@ -10,6 +10,7 @@
 TREATIES = 1024
 YEAR_DEV = 32
 TAIL = 16
+CHUNKS = 4
 LANES = 128
 SUBLANES = 8
 UNIT_LOSS = 1.0
@@ -82,34 +83,39 @@
     return total[0:1]
 
 
-def kernel(
-    sizes,
-    loss_ref,
-    year_ref,
-    retention_ref,
-    risk_ref,
-    share_ref,
-    member_ref,
-    attach_ref,
-    limit_ref,
-    reinst_ref,
-    rate_ref,
-    stop_attach_ref,
-    stop_width_ref,
-    net_ref,
-    stop_ref,
-    tail_ref,
-    ceded,
-    sending,
-    landing,
-    held,
-    own_sum,
-    kept,
-    port_send,
-    port_recv,
-    year_send,
-    year_recv,
-):
+def kernel(sizes, *refs):
+    sources = refs[:12]
+    net_ref, stop_ref, tail_ref = refs[12:15]
+    inputs = refs[15:27]
+    (
+        loss_ref,
+        year_ref,
+        retention_ref,
+        risk_ref,
+        share_ref,
+        member_ref,
+        attach_ref,
+        limit_ref,
+        reinst_ref,
+        rate_ref,
+        stop_attach_ref,
+        stop_width_ref,
+    ) = inputs
+    (
+        weight,
+        ceded,
+        sending,
+        landing,
+        held,
+        own_sum,
+        kept,
+        loss_sem,
+        input_sem,
+        port_send,
+        port_recv,
+        year_send,
+        year_recv,
+    ) = refs[27:]
     n_year, n_port, own, groups = sizes
     rows, ports = loss_ref.shape
     me_port = lax.axis_index("port")
@@ -123,11 +129,30 @@
         peer = lax.rem(me_year + step, n_year)
         pl.semaphore_signal(barrier, inc=1, device_id={"year": peer}, device_id_type=MESH)
 
-    ceded[...] = clamp_between(
-        loss_ref[...].astype(jnp.float32) - retention_ref[...], 0.0, risk_ref[...]
-    ).astype(jnp.bfloat16)
-
-    def product(dest, group):
+    chunk_rows = rows // CHUNKS
+
+    def chunk(index):
+        return slice(index * chunk_rows, (index + 1) * chunk_rows)
+
+    def load(index):
+        return pltpu.make_async_copy(sources[index], inputs[index], input_sem.at[index])
+
+    def load_losses(index):
+        return pltpu.make_async_copy(
+            sources[0].at[chunk(index)], loss_ref.at[chunk(index)], loss_sem.at[index]
+        )
+
+    for index in (5, 4):
+        load(index).start()
+    load_losses(0).start()
+    for index in (2, 3):
+        load(index).start()
+    for index in range(1, CHUNKS):
+        load_losses(index).start()
+    for index in (1, 6, 7, 8, 9, 10, 11):
+        load(index).start()
+
+    def set_weights(dest, group):
         lane = lax.broadcasted_iota(jnp.int32, (LANES, ports), 0) + group * LANES
         treaty = lane + dest * own
         if own % LANES:
@@ -139,91 +164,120 @@
                 share_ref[slot : slot + 1, :].astype(jnp.float32),
                 weights,
             )
+        weight[...] = weights.astype(jnp.bfloat16)
+
+    def weighted(losses):
         return lax.dot_general(
-            ceded[...],
-            weights.astype(jnp.bfloat16),
+            losses,
+            weight[...],
             (((1,), (1,)), ((), ())),
             preferred_element_type=jnp.float32,
         )
 
-    def port_copy(piece, group, device, slot):
+    def product(dest, group):
+        set_weights(dest, group)
+        return weighted(ceded[...])
+
+    def cede(index):
+        load_losses(index).wait()
+        if index == 0:
+            load(2).wait()
+            load(3).wait()
+        part = chunk(index)
+        ceded[part] = clamp_between(
+            loss_ref[part].astype(jnp.float32) - retention_ref[...], 0.0, risk_ref[...]
+        ).astype(jnp.bfloat16)
+
+    def port_copy(piece, group, index, device, slot):
         return pltpu.make_async_remote_copy(
-            src_ref=sending.at[piece, group],
-            dst_ref=landing.at[slot, group],
-            send_sem=port_send.at[piece, group],
-            recv_sem=port_recv.at[slot, group],
+            src_ref=sending.at[piece, group, chunk(index)],
+            dst_ref=landing.at[slot, group, chunk(index)],
+            send_sem=port_send.at[piece, group, index],
+            recv_sem=port_recv.at[slot, group, index],
             device_id={"port": device},
             device_id_type=MESH,
         )
 
-    def wait_landed(slot, group):
-        port_copy(0, group, me_port, slot).wait_recv()
-
-    waited = []
-
-    def entered():
-        if not waited:
-            pl.semaphore_wait(barrier, n_port + n_year - 2)
-            waited.append(True)
+    def wait_landed(slot, group, index):
+        port_copy(0, group, index, me_port, slot).wait_recv()
 
     copies = []
+
+    def send(piece, group, index, device, slot):
+        copy = port_copy(piece, group, index, device, slot)
+        copy.start()
+        copies.append(copy)
+
+    def send_first(dest, device, slot):
+        load(5).wait()
+        load(4).wait()
+        set_weights(dest, 0)
+        for index in range(CHUNKS):
+            cede(index)
+            sending[0, 0, chunk(index)] = weighted(ceded[chunk(index)]).astype(jnp.bfloat16)
+            if index == 0:
+                pl.semaphore_wait(barrier, n_port + n_year - 2)
+            send(0, 0, index, device, slot)
+
+    def send_piece(piece, group, dest, device, slot):
+        sending[piece, group] = product(dest, group).astype(jnp.bfloat16)
+        for index in range(CHUNKS):
+            send(piece, group, index, device, slot)
+
     if n_port == 4:
         is_end = (me_port == 0) | (me_port == 3)
         near = me_port + 1 - 2 * lax.rem(me_port, 2)
         low_half = me_port < 2
         far_end = jnp.where(low_half, 3, 0)
         far_middle = jnp.where(low_half, 2, 1)
+        first_dest = jnp.where(is_end, far_middle, far_end)
+        first_device = jnp.where(is_end, near, far_end)
+        second_dest = jnp.where(is_end, far_end, near)
+        last_dest = jnp.where(is_end, near, far_middle)
+        last_slot = jnp.where(is_end, 0, 1)
         for group in range(groups):
-            dest = jnp.where(is_end, far_middle, far_end)
-            sending[0, group] = product(dest, group).astype(jnp.bfloat16)
-            entered()
-            copy = port_copy(0, group, jnp.where(is_end, near, far_end), 2)
-            copy.start()
-            copies.append(copy)
-
-            dest = jnp.where(is_end, far_end, near)
-            sending[1, group] = product(dest, group).astype(jnp.bfloat16)
-            copy = port_copy(1, group, dest, jnp.where(is_end, 1, 0))
-            copy.start()
-            copies.append(copy)
-
-            last = product(jnp.where(is_end, near, far_middle), group)
-            held[group] = last
-            copy = port_copy(
-                2, group, jnp.where(is_end, near, far_middle), jnp.where(is_end, 0, 1)
-            )
-            copies.append(copy)
+            if group == 0:
+                send_first(first_dest, first_device, 2)
+            else:
+                send_piece(0, group, first_dest, first_device, 2)
+            send_piece(1, group, second_dest, second_dest, jnp.where(is_end, 1, 0))
+            held[group] = product(last_dest, group)
 
             @pl.when(is_end)
             def _():
                 sending[2, group] = held[group].astype(jnp.bfloat16)
-                copy.start()
+                for index in range(CHUNKS):
+                    port_copy(2, group, index, last_dest, last_slot).start()
 
         for group in range(groups):
             own_sum[group] = product(me_port, group)
         for group in range(groups):
-            copy = copies[3 * group + 2]
 
             @pl.when(jnp.logical_not(is_end))
             def _():
-                wait_landed(2, group)
-                sending[2, group] = (
-                    held[group] + landing[2, group].astype(jnp.float32)
-                ).astype(jnp.bfloat16)
-                copy.start()
+                for index in range(CHUNKS):
+                    wait_landed(2, group, index)
+                    part = chunk(index)
+                    sending[2, group, part] = (
+                        held[group, part] + landing[2, group, part].astype(jnp.float32)
+                    ).astype(jnp.bfloat16)
+                    port_copy(2, group, index, last_dest, last_slot).start()
+
+            for index in range(CHUNKS):
+                copies.append(port_copy(2, group, index, last_dest, last_slot))
 
     else:
         for group in range(groups):
             for step in range(1, n_port):
                 dest = lax.rem(me_port + step, n_port)
-                sending[step - 1, group] = product(dest, group).astype(jnp.bfloat16)
-                entered()
-                copy = port_copy(step - 1, group, dest, step - 1)
-                copy.start()
-                copies.append(copy)
+                if group == 0 and step == 1:
+                    send_first(dest, dest, 0)
+                else:
+                    send_piece(step - 1, group, dest, dest, step - 1)
         for group in range(groups):
             own_sum[group] = product(me_port, group)
-    entered()
+    for index in (1, 6, 7, 8, 9, 10, 11):
+        load(index).wait()
 
     local_year = year_ref[...] - me_year * YEAR_DEV
     hits = (
@@ -253,12 +307,14 @@
         lanes = slice(group * LANES, (group + 1) * LANES)
         event_treaty = own_sum[group]
         if n_port == 4:
-            wait_landed(0, group)
-            wait_landed(1, group)
+            for index in range(CHUNKS):
+                wait_landed(0, group, index)
+                wait_landed(1, group, index)
 
             @pl.when(is_end)
             def _():
-                wait_landed(2, group)
+                for index in range(CHUNKS):
+                    wait_landed(2, group, index)
 
             event_treaty = event_treaty + landing[0, group].astype(jnp.float32)
             event_treaty = event_treaty + landing[1, group].astype(jnp.float32)
@@ -267,7 +323,8 @@
             )
         else:
             for slot in range(n_port - 1):
-                wait_landed(slot, group)
+                for index in range(CHUNKS):
+                    wait_landed(slot, group, index)
                 event_treaty = event_treaty + landing[slot, group].astype(jnp.float32)
         attach = attach_ref[:, lanes].astype(jnp.float32) * UNIT_LOSS
         limit_loss = limit_ref[:, lanes].astype(jnp.float32) * UNIT_LOSS
@@ -311,6 +368,18 @@
         copy.wait_send()
 
 
+def put_out(*refs):
+    results, outputs, sem = refs[:3], refs[3:6], refs[6]
+    moves = [
+        pltpu.make_async_copy(result, output, sem.at[index])
+        for index, (result, output) in enumerate(zip(results, outputs))
+    ]
+    for move in moves:
+        move.start()
+    for move in moves:
+        move.wait()
+
+
 def on_device(sizes, event_loss, event_year, retention, risk_limit, share, member, *terms):
     n_year, n_port, own, groups = sizes
     rows, ports = event_loss.shape
@@ -324,32 +393,7 @@
             values = jnp.pad(values, (0, padded - own), constant_values=1)
         return row(values)
 
-    vmem = pl.BlockSpec(memory_space=pltpu.VMEM)
-    pieces = n_port - 1
-    layer_net, stop_loss, tail_mean = pl.pallas_call(
-        functools.partial(kernel, sizes),
-        name="layers",
-        out_shape=(
-            jax.ShapeDtypeStruct((YEAR_DEV, padded), jnp.float32),
-            jax.ShapeDtypeStruct((YEAR_DEV, padded), jnp.float32),
-            jax.ShapeDtypeStruct((1, padded), jnp.float32),
-        ),
-        in_specs=[vmem] * 12,
-        out_specs=(vmem, vmem, vmem),
-        scratch_shapes=[
-            pltpu.VMEM((rows, ports), jnp.bfloat16),
-            pltpu.VMEM((pieces, groups, rows, LANES), jnp.bfloat16),
-            pltpu.VMEM((pieces, groups, rows, LANES), jnp.bfloat16),
-            pltpu.VMEM((groups, rows, LANES), jnp.float32),
-            pltpu.VMEM((groups, rows, LANES), jnp.float32),
-            pltpu.VMEM((groups, n_year, YEAR_DEV, LANES), jnp.float32),
-            pltpu.SemaphoreType.DMA((pieces, groups)),
-            pltpu.SemaphoreType.DMA((pieces, groups)),
-            pltpu.SemaphoreType.DMA((groups, n_year)),
-            pltpu.SemaphoreType.DMA((groups, n_year)),
-        ],
-        compiler_params=pltpu.CompilerParams(collective_id=0, has_side_effects=True),
-    )(
+    operands = [
         event_loss,
         row(event_year),
         row(retention),
@@ -357,7 +401,43 @@
         share.T,
         member.T,
         *[term_row(values) for values in terms],
-    )
+    ]
+    anywhere = pl.BlockSpec(memory_space=pl.ANY)
+    vmem = pl.BlockSpec(memory_space=pltpu.VMEM)
+    pieces = n_port - 1
+    shapes = [(YEAR_DEV, padded), (YEAR_DEV, padded), (1, padded)]
+    results = pl.pallas_call(
+        functools.partial(kernel, sizes),
+        name="layers",
+        out_shape=[pltpu.VMEM(shape, jnp.float32) for shape in shapes],
+        in_specs=[anywhere] * len(operands),
+        out_specs=[vmem] * len(shapes),
+        scratch_shapes=[
+            *[pltpu.VMEM(operand.shape, operand.dtype) for operand in operands],
+            pltpu.VMEM((LANES, ports), jnp.bfloat16),
+            pltpu.VMEM((rows, ports), jnp.bfloat16),
+            pltpu.VMEM((pieces, groups, rows, LANES), jnp.bfloat16),
+            pltpu.VMEM((pieces, groups, rows, LANES), jnp.bfloat16),
+            pltpu.VMEM((groups, rows, LANES), jnp.float32),
+            pltpu.VMEM((groups, rows, LANES), jnp.float32),
+            pltpu.VMEM((groups, n_year, YEAR_DEV, LANES), jnp.float32),
+            pltpu.SemaphoreType.DMA((CHUNKS,)),
+            pltpu.SemaphoreType.DMA((len(operands),)),
+            pltpu.SemaphoreType.DMA((pieces, groups, CHUNKS)),
+            pltpu.SemaphoreType.DMA((pieces, groups, CHUNKS)),
+            pltpu.SemaphoreType.DMA((groups, n_year)),
+            pltpu.SemaphoreType.DMA((groups, n_year)),
+        ],
+        compiler_params=pltpu.CompilerParams(collective_id=0, has_side_effects=True),
+    )(*operands)
+    layer_net, stop_loss, tail_mean = pl.pallas_call(
+        put_out,
+        name="put_out",
+        out_shape=[jax.ShapeDtypeStruct(shape, jnp.float32) for shape in shapes],
+        in_specs=[anywhere] * len(shapes),
+        out_specs=[anywhere] * len(shapes),
+        scratch_shapes=[pltpu.SemaphoreType.DMA((len(shapes),))],
+    )(*[pltpu.with_memory_space_constraint(value, pltpu.VMEM) for value in results])
     return layer_net[:, :own].T, stop_loss[:, :own].T, tail_mean[0, :own]
 
 

time: 33.4 us -> 30.2 us (0.904)
  local copies, waits for them, and re-layouts: 2.63 us -> 0 us
  Pallas kernels: 29.9 us -> 29.3 us
    unnamed x7 -> x0, local copies, waits for them, and re-layouts: 2.63 us -> none
    pallas_call x1, Pallas kernels: 29.9 us -> 28.6 us  [on_device(): pl.pallas_call(functools.partial(kernel, sizes), name='layers', out_shape...]
    pallas_call x0 -> x1, Pallas kernels: none -> 0.66 us  [on_device(): pl.pallas_call(put_out, name='put_out', out_shape=[jax.ShapeDtypeStruct(s...]
where the time goes in v2:
time: 30.2 us; the launch traced here: 29.9 us
  Pallas kernels  29.3 us (97%)
  between operations  0.64 us (2%)
    pallas_call x1, Pallas kernels, on_device(): pl.pallas_call(functools.partial(kernel, sizes), name='layers', out_shape...  28.6 us
    pallas_call x1, Pallas kernels, on_device(): pl.pallas_call(put_out, name='put_out', out_shape=[jax.ShapeDtypeStruct(s...  0.66 us

profile of v2, /device:TPU:0, one launch (start us, length us, event | category | flops | bytes accessed | tf_op | source)
XLA Modules:
  0.0 29.9 jit_solution(17292266098618487742)
XLA Ops:
  0.6 28.6 %layers.1 = (f32[32,256]{1,0:T(8,128)S(1)}, f32[32,256]{1,0:T(8,128)S(1)}, f32[1,256]{1,0:T(1,128)S(1)}) custom-call(bf16[512,1024]{1,0:T(8,128)(2,1)} %refs_0_.1, s32[1,512]{1,0:T(1,128)} %bitcast.18, f32[1,1024]{1,0:T(1,128)} %bitcast.16, f32[1,1024]{1,0:T(1,128)} %bitcast.17, bf16[4,1024]{1,0:T(4,128)(2,1)} %bitcast.15, s32[4,1024]{1,0:T(4,128)} %bitcast.14, ...), custom_call_target="tpu_custom_call" | custom-call | tf_op jit(solution)/shard_map/layers/pallas_call | solution.py:409
  29.3 0.7 %put_out.1 = (f32[32,256]{1,0:T(8,128)}, f32[32,256]{1,0:T(8,128)}, f32[1,256]{1,0:T(1,128)}) custom-call(f32[32,256]{1,0:T(8,128)S(1)} %get-tuple-element.9.refs_0_, f32[32,256]{1,0:T(8,128)S(1)} %get-tuple-element.10.refs_1_, f32[1,256]{1,0:T(1,128)S(1)} %get-tuple-element.11.refs_2_), custom_call_target="tpu_custom_call" | custom-call | tf_op jit(solution)/shard_map/put_out/pallas_call | solution.py:433

commit v3 on v2

--- a/solution.py
+++ b/solution.py
@@ -102,6 +102,9 @@
         stop_width_ref,
     ) = inputs
     (
+        terms,
+        given,
+        adopted,
         weight,
         ceded,
         sending,
@@ -109,6 +112,7 @@
         held,
         own_sum,
         kept,
+        hand_sem,
         loss_sem,
         input_sem,
         port_send,
@@ -188,184 +192,224 @@
             loss_ref[part].astype(jnp.float32) - retention_ref[...], 0.0, risk_ref[...]
         ).astype(jnp.bfloat16)
 
-    def port_copy(piece, group, index, device, slot):
+    def port_copy(piece, index, device, slot):
         return pltpu.make_async_remote_copy(
-            src_ref=sending.at[piece, group, chunk(index)],
-            dst_ref=landing.at[slot, group, chunk(index)],
-            send_sem=port_send.at[piece, group, index],
-            recv_sem=port_recv.at[slot, group, index],
+            src_ref=sending.at[piece, chunk(index)],
+            dst_ref=landing.at[slot, chunk(index)],
+            send_sem=port_send.at[piece, index],
+            recv_sem=port_recv.at[slot, index],
             device_id={"port": device},
             device_id_type=MESH,
         )
 
-    def wait_landed(slot, group, index):
-        port_copy(0, group, index, me_port, slot).wait_recv()
-
-    copies = []
-
-    def send(piece, group, index, device, slot):
-        copy = port_copy(piece, group, index, device, slot)
+    def hand_copy(which, source, target, device):
+        return pltpu.make_async_remote_copy(
+            src_ref=source,
+            dst_ref=target,
+            send_sem=hand_sem.at[which, 0],
+            recv_sem=hand_sem.at[which, 1],
+            device_id={"port": device},
+            device_id_type=MESH,
+        )
+
+    def wait_landed(slot, index):
+        port_copy(0, index, me_port, slot).wait_recv()
+
+    def send(copies, piece, index, device, slot):
+        copy = port_copy(piece, index, device, slot)
         copy.start()
         copies.append(copy)
 
-    def send_first(dest, device, slot):
+    def send_first(copies, dest, group, device, slot):
         load(5).wait()
         load(4).wait()
-        set_weights(dest, 0)
+        set_weights(dest, group)
         for index in range(CHUNKS):
             cede(index)
-            sending[0, 0, chunk(index)] = weighted(ceded[chunk(index)]).astype(jnp.bfloat16)
+            sending[0, chunk(index)] = weighted(ceded[chunk(index)]).astype(jnp.bfloat16)
             if index == 0:
                 pl.semaphore_wait(barrier, n_port + n_year - 2)
-            send(0, 0, index, device, slot)
-
-    def send_piece(piece, group, dest, device, slot):
-        sending[piece, group] = product(dest, group).astype(jnp.bfloat16)
+            send(copies, 0, index, device, slot)
+
+    def send_piece(copies, piece, dest, group, device, slot):
+        sending[piece] = product(dest, group).astype(jnp.bfloat16)
         for index in range(CHUNKS):
-            send(piece, group, index, device, slot)
-
-    if n_port == 4:
-        is_end = (me_port == 0) | (me_port == 3)
-        near = me_port + 1 - 2 * lax.rem(me_port, 2)
-        low_half = me_port < 2
-        far_end = jnp.where(low_half, 3, 0)
-        far_middle = jnp.where(low_half, 2, 1)
-        first_dest = jnp.where(is_end, far_middle, far_end)
-        first_device = jnp.where(is_end, near, far_end)
-        second_dest = jnp.where(is_end, far_end, near)
-        last_dest = jnp.where(is_end, near, far_middle)
-        last_slot = jnp.where(is_end, 0, 1)
+            send(copies, piece, index, device, slot)
+
+    def merge(copies, store, landed, piece, device, slot):
+        for index in range(CHUNKS):
+            wait_landed(landed, index)
+            part = chunk(index)
+            sending[piece, part] = (
+                held[store, part] + landing[landed, part].astype(jnp.float32)
+            ).astype(jnp.bfloat16)
+            send(copies, piece, index, device, slot)
+
+    def gather_terms():
+        for index in (1, 6, 7, 8, 9, 10, 11):
+            load(index).wait()
         for group in range(groups):
-            if group == 0:
-                send_first(first_dest, first_device, 2)
-            else:
-                send_piece(0, group, first_dest, first_device, 2)
-            send_piece(1, group, second_dest, second_dest, jnp.where(is_end, 1, 0))
-            held[group] = product(last_dest, group)
-
-            @pl.when(is_end)
-            def _():
-                sending[2, group] = held[group].astype(jnp.bfloat16)
-                for index in range(CHUNKS):
-                    port_copy(2, group, index, last_dest, last_slot).start()
-
-        for group in range(groups):
-            own_sum[group] = product(me_port, group)
-        for group in range(groups):
-
-            @pl.when(jnp.logical_not(is_end))
-            def _():
-                for index in range(CHUNKS):
-                    wait_landed(2, group, index)
-                    part = chunk(index)
-                    sending[2, group, part] = (
-                        held[group, part] + landing[2, group, part].astype(jnp.float32)
-                    ).astype(jnp.bfloat16)
-                    port_copy(2, group, index, last_dest, last_slot).start()
-
-            for index in range(CHUNKS):
-                copies.append(port_copy(2, group, index, last_dest, last_slot))
-
-    else:
-        for group in range(groups):
-            for step in range(1, n_port):
-                dest = lax.rem(me_port + step, n_port)
-                if group == 0 and step == 1:
-                    send_first(dest, dest, 0)
-                else:
-                    send_piece(step - 1, group, dest, dest, step - 1)
-        for group in range(groups):
-            own_sum[group] = product(me_port, group)
-    for index in (1, 6, 7, 8, 9, 10, 11):
-        load(index).wait()
-
-    local_year = year_ref[...] - me_year * YEAR_DEV
-    hits = (
-        (local_year == lax.broadcasted_iota(jnp.int32, (YEAR_DEV, rows), 0))
-        .astype(jnp.float32)
-        .astype(jnp.bfloat16)
-    )
+            for place, ref in enumerate(inputs[6:12]):
+                terms[group, place : place + 1, :] = ref[:, lanes_of(group)].astype(jnp.float32)
+            terms[group, 6:8, :] = jnp.ones((2, LANES), jnp.float32)
+
+    def lanes_of(group):
+        return slice(group * LANES, (group + 1) * LANES)
+
+    def term(group, place):
+        return terms[group, place : place + 1, :]
 
     def split_dot(values):
+        local_year = year_ref[...] - me_year * YEAR_DEV
+        hits = (
+            (local_year == lax.broadcasted_iota(jnp.int32, (YEAR_DEV, rows), 0))
+            .astype(jnp.float32)
+            .astype(jnp.bfloat16)
+        )
         upper = values.astype(jnp.bfloat16)
         lower = (values - upper.astype(jnp.float32)).astype(jnp.bfloat16)
         return jnp.dot(hits, upper, preferred_element_type=jnp.float32) + jnp.dot(
             hits, lower, preferred_element_type=jnp.float32
         )
 
-    def year_copy(step, group):
+    def year_copy(place, step, owner):
         return pltpu.make_async_remote_copy(
-            src_ref=kept.at[group, me_year],
-            dst_ref=kept.at[group, me_year],
-            send_sem=year_send.at[group, step - 1],
-            recv_sem=year_recv.at[group, me_year],
+            src_ref=kept.at[place, owner],
+            dst_ref=kept.at[place, owner],
+            send_sem=year_send.at[place, step - 1],
+            recv_sem=year_recv.at[place, owner],
             device_id={"year": lax.rem(me_year + step, n_year)},
             device_id_type=MESH,
         )
 
-    for group in range(groups):
-        lanes = slice(group * LANES, (group + 1) * LANES)
-        event_treaty = own_sum[group]
-        if n_port == 4:
+    def year_stage(copies, place, slots, group):
+        event_treaty = own_sum[place]
+        for slot in slots:
             for index in range(CHUNKS):
-                wait_landed(0, group, index)
-                wait_landed(1, group, index)
-
-            @pl.when(is_end)
-            def _():
-                for index in range(CHUNKS):
-                    wait_landed(2, group, index)
-
-            event_treaty = event_treaty + landing[0, group].astype(jnp.float32)
-            event_treaty = event_treaty + landing[1, group].astype(jnp.float32)
-            event_treaty = event_treaty + jnp.where(
-                is_end, landing[2, group].astype(jnp.float32), 0.0
-            )
-        else:
-            for slot in range(n_port - 1):
-                for index in range(CHUNKS):
-                    wait_landed(slot, group, index)
-                event_treaty = event_treaty + landing[slot, group].astype(jnp.float32)
-        attach = attach_ref[:, lanes].astype(jnp.float32) * UNIT_LOSS
-        limit_loss = limit_ref[:, lanes].astype(jnp.float32) * UNIT_LOSS
+                wait_landed(slot, index)
+            event_treaty = event_treaty + landing[slot].astype(jnp.float32)
+        attach = term(group, 0) * UNIT_LOSS
+        limit_loss = term(group, 1) * UNIT_LOSS
         recovered = clamp_between(event_treaty - attach, 0.0, limit_loss)
         retained = event_treaty - recovered
         yearly = split_dot(jnp.concatenate((recovered, retained), 1))
         annual = yearly[:, :LANES]
-        kept[group, me_year] = yearly[:, LANES:]
+        kept[place, me_year] = yearly[:, LANES:]
         for step in range(1, n_year):
-            copy = year_copy(step, group)
+            copy = year_copy(place, step, me_year)
             copy.start()
             copies.append(copy)
-        reinstated = reinst_ref[:, lanes].astype(jnp.float32)
+        reinstated = term(group, 2)
         layer_paid = jnp.minimum(annual, (1.0 + reinstated) * limit_loss)
-        net_ref[:, lanes] = (
-            layer_paid
-            - rate_ref[:, lanes] * jnp.minimum(layer_paid, reinstated * limit_loss)
+        return (
+            layer_paid - term(group, 3) * jnp.minimum(layer_paid, reinstated * limit_loss)
         ) / limit_loss
 
-    for group in range(groups):
-        lanes = slice(group * LANES, (group + 1) * LANES)
+    def last_stage(place, group):
         for step in range(1, n_year):
-            source = lax.rem(me_year + step, n_year)
-            pltpu.make_async_remote_copy(
-                src_ref=kept.at[group, source],
-                dst_ref=kept.at[group, source],
-                send_sem=year_send.at[group, step - 1],
-                recv_sem=year_recv.at[group, source],
-                device_id={"year": source},
-                device_id_type=MESH,
-            ).wait_recv()
-        every = kept[group].reshape(n_year * YEAR_DEV, LANES)
+            year_copy(place, step, lax.rem(me_year + step, n_year)).wait_recv()
+        every = kept[place].reshape(n_year * YEAR_DEV, LANES)
         base_loss = UNIT_LOSS + jnp.sum(every, axis=0, keepdims=True) / (n_year * YEAR_DEV)
-        tail_ref[:, lanes] = largest_sum(every) / base_loss / TAIL
-        loss_ratio = kept[group, me_year] / base_loss
-        stop_ref[:, lanes] = clamp_between(
-            loss_ratio - stop_attach_ref[:, lanes], 0.0, stop_width_ref[:, lanes]
-        )
-
-    for copy in copies:
-        copy.wait_send()
+        tail = largest_sum(every) / base_loss / TAIL
+        loss_ratio = kept[place, me_year] / base_loss
+        return clamp_between(loss_ratio - term(group, 4), 0.0, term(group, 5)), tail
+
+    def finish(copies):
+        for copy in copies:
+            copy.wait_send()
+
+    if balanced(n_port, groups):
+        is_end = (me_port == 0) | (me_port == 3)
+        low_half = me_port < 2
+        near_end = jnp.where(low_half, 0, 3)
+        near_middle = jnp.where(low_half, 1, 2)
+        far_end = 3 - near_end
+        far_middle = 3 - near_middle
+
+        @pl.when(is_end)
+        def _():
+            copies = []
+            send_first(copies, far_middle, 0, near_middle, 0)
+            send_piece(copies, 1, far_end, 0, near_middle, 1)
+            send_piece(copies, 2, far_end, 1, near_middle, 2)
+            send_piece(copies, 3, far_middle, 1, near_middle, 3)
+            send_piece(copies, 4, near_middle, 1, near_middle, 4)
+            own_sum[0] = product(near_middle, 0)
+            own_sum[1] = product(near_end, 0)
+            own_sum[2] = product(near_end, 1)
+            gather_terms()
+            hand_copy(0, terms.at[0], terms.at[groups], me_port).wait_recv()
+            adopted_net = year_stage(copies, 0, (0,), groups)
+            net_ref[:, lanes_of(0)] = year_stage(copies, 1, (1, 2), 0)
+            adopted_stop, adopted_tail = last_stage(0, groups)
+            given[0:YEAR_DEV] = adopted_net
+            given[YEAR_DEV : 2 * YEAR_DEV] = adopted_stop
+            given[2 * YEAR_DEV :] = jnp.broadcast_to(adopted_tail, (SUBLANES, LANES))
+            hand_over = hand_copy(1, given, adopted, near_middle)
+            hand_over.start()
+            copies.append(hand_over)
+            net_ref[:, lanes_of(1)] = year_stage(copies, 2, (3, 4), 1)
+            for group in range(groups):
+                stop_loss, tail = last_stage(1 + group, group)
+                stop_ref[:, lanes_of(group)] = stop_loss
+                tail_ref[:, lanes_of(group)] = tail
+            finish(copies)
+
+        @pl.when(jnp.logical_not(is_end))
+        def _():
+            copies = []
+            send_first(copies, near_end, 0, near_end, 2)
+            gather_terms()
+            hand_over = hand_copy(0, terms.at[0], terms.at[groups], near_end)
+            hand_over.start()
+            copies.append(hand_over)
+            send_piece(copies, 1, near_end, 1, near_end, 4)
+            held[0] = product(far_middle, 0)
+            held[1] = product(far_end, 0)
+            held[2] = product(near_middle, 0)
+            merge(copies, 0, 0, 2, far_middle, 5)
+            held[3] = product(far_end, 1)
+            held[4] = product(far_middle, 1)
+            merge(copies, 1, 1, 3, far_end, 1)
+            own_sum[0] = product(near_middle, 1)
+            merge(copies, 2, 5, 4, near_end, 0)
+            merge(copies, 3, 2, 5, far_end, 3)
+            merge(copies, 4, 3, 6, far_middle, 6)
+            net_ref[:, lanes_of(1)] = year_stage(copies, 0, (6, 4), 1)
+            hand_copy(1, given, adopted, me_port).wait_recv()
+            net_ref[:, lanes_of(0)] = adopted[0:YEAR_DEV]
+            stop_ref[:, lanes_of(0)] = adopted[YEAR_DEV : 2 * YEAR_DEV]
+            tail_ref[:, lanes_of(0)] = adopted[2 * YEAR_DEV : 2 * YEAR_DEV + 1]
+            stop_loss, tail = last_stage(0, 1)
+            stop_ref[:, lanes_of(1)] = stop_loss
+            tail_ref[:, lanes_of(1)] = tail
+            finish(copies)
+
+    else:
+        copies = []
+        for group in range(groups):
+            for step in range(1, n_port):
+                dest = lax.rem(me_port + step, n_port)
+                slot = (step - 1) * groups + group
+                if slot == 0:
+                    send_first(copies, dest, group, dest, slot)
+                else:
+                    send_piece(copies, slot, dest, group, dest, slot)
+        for group in range(groups):
+            own_sum[group] = product(me_port, group)
+        gather_terms()
+        for group in range(groups):
+            slots = [step * groups + group for step in range(n_port - 1)]
+            net_ref[:, lanes_of(group)] = year_stage(copies, group, slots, group)
+        for group in range(groups):
+            stop_loss, tail = last_stage(group, group)
+            stop_ref[:, lanes_of(group)] = stop_loss
+            tail_ref[:, lanes_of(group)] = tail
+        finish(copies)
+
+
+def balanced(n_port, groups):
+    return n_port == 4 and groups == 2
 
 
 def put_out(*refs):
@@ -404,7 +448,10 @@
     ]
     anywhere = pl.BlockSpec(memory_space=pl.ANY)
     vmem = pl.BlockSpec(memory_space=pltpu.VMEM)
-    pieces = n_port - 1
+    if balanced(n_port, groups):
+        pieces, places, stores = 7, groups + 1, 5
+    else:
+        pieces, places, stores = (n_port - 1) * groups, groups, 1
     shapes = [(YEAR_DEV, padded), (YEAR_DEV, padded), (1, padded)]
     results = pl.pallas_call(
         functools.partial(kernel, sizes),
@@ -414,19 +461,23 @@
         out_specs=[vmem] * len(shapes),
         scratch_shapes=[
             *[pltpu.VMEM(operand.shape, operand.dtype) for operand in operands],
+            pltpu.VMEM((groups + 1, SUBLANES, LANES), jnp.float32),
+            pltpu.VMEM((2 * YEAR_DEV + SUBLANES, LANES), jnp.float32),
+            pltpu.VMEM((2 * YEAR_DEV + SUBLANES, LANES), jnp.float32),
             pltpu.VMEM((LANES, ports), jnp.bfloat16),
             pltpu.VMEM((rows, ports), jnp.bfloat16),
-            pltpu.VMEM((pieces, groups, rows, LANES), jnp.bfloat16),
-            pltpu.VMEM((pieces, groups, rows, LANES), jnp.bfloat16),
-            pltpu.VMEM((groups, rows, LANES), jnp.float32),
-            pltpu.VMEM((groups, rows, LANES), jnp.float32),
-            pltpu.VMEM((groups, n_year, YEAR_DEV, LANES), jnp.float32),
+            pltpu.VMEM((pieces, rows, LANES), jnp.bfloat16),
+            pltpu.VMEM((pieces, rows, LANES), jnp.bfloat16),
+            pltpu.VMEM((stores, rows, LANES), jnp.float32),
+            pltpu.VMEM((places, rows, LANES), jnp.float32),
+            pltpu.VMEM((places, n_year, YEAR_DEV, LANES), jnp.float32),
+            pltpu.SemaphoreType.DMA((2, 2)),
             pltpu.SemaphoreType.DMA((CHUNKS,)),
             pltpu.SemaphoreType.DMA((len(operands),)),
-            pltpu.SemaphoreType.DMA((pieces, groups, CHUNKS)),
-            pltpu.SemaphoreType.DMA((pieces, groups, CHUNKS)),
-            pltpu.SemaphoreType.DMA((groups, n_year)),
-            pltpu.SemaphoreType.DMA((groups, n_year)),
+            pltpu.SemaphoreType.DMA((pieces, CHUNKS)),
+            pltpu.SemaphoreType.DMA((pieces, CHUNKS)),
+            pltpu.SemaphoreType.DMA((places, n_year)),
+            pltpu.SemaphoreType.DMA((places, n_year)),
         ],
         compiler_params=pltpu.CompilerParams(collective_id=0, has_side_effects=True),
     )(*operands)

time: 30.2 us -> 32.9 us (1.089)
  Pallas kernels: 29.3 us -> 32.1 us
    pallas_call x1, Pallas kernels: 28.6 us -> 31.4 us  [on_device(): pl.pallas_call(functools.partial(kernel, sizes), name='layers', out_shape...]
where the time goes in v3:
time: 32.9 us; the launch traced here: 32.7 us
  Pallas kernels  32.1 us (98%)
  between operations  0.64 us (2%)
    pallas_call x1, Pallas kernels, on_device(): pl.pallas_call(functools.partial(kernel, sizes), name='layers', out_shape...  31.4 us

profile of v3, /device:TPU:0, one launch (start us, length us, event | category | flops | bytes accessed | tf_op | source)
XLA Modules:
  0.0 32.7 jit_solution(9665946557425115622)
XLA Ops:
  0.6 31.4 %layers.1 = (f32[32,256]{1,0:T(8,128)S(1)}, f32[32,256]{1,0:T(8,128)S(1)}, f32[1,256]{1,0:T(1,128)S(1)}) custom-call(bf16[512,1024]{1,0:T(8,128)(2,1)} %refs_0_.1, s32[1,512]{1,0:T(1,128)} %bitcast.18, f32[1,1024]{1,0:T(1,128)} %bitcast.16, f32[1,1024]{1,0:T(1,128)} %bitcast.17, bf16[4,1024]{1,0:T(4,128)(2,1)} %bitcast.15, s32[4,1024]{1,0:T(4,128)} %bitcast.14, ...), custom_call_target="tpu_custom_call" | custom-call | tf_op jit(solution)/shard_map/layers/pallas_call | solution.py:456
  32.0 0.7 %put_out.1 = (f32[32,256]{1,0:T(8,128)}, f32[32,256]{1,0:T(8,128)}, f32[1,256]{1,0:T(1,128)}) custom-call(f32[32,256]{1,0:T(8,128)S(1)} %get-tuple-element.9.refs_0_, f32[32,256]{1,0:T(8,128)S(1)} %get-tuple-element.10.refs_1_, f32[1,256]{1,0:T(1,128)S(1)} %get-tuple-element.11.refs_2_), custom_call_target="tpu_custom_call" | custom-call | tf_op jit(solution)/shard_map/put_out/pallas_call | solution.py:484

commit v4 on v2

--- a/solution.py
+++ b/solution.py
@@ -121,14 +121,6 @@
     me_port = lax.axis_index("port")
     me_year = lax.axis_index("year")
 
-    barrier = pltpu.get_barrier_semaphore()
-    for step in range(1, n_port):
-        peer = lax.rem(me_port + step, n_port)
-        pl.semaphore_signal(barrier, inc=1, device_id={"port": peer}, device_id_type=MESH)
-    for step in range(1, n_year):
-        peer = lax.rem(me_year + step, n_year)
-        pl.semaphore_signal(barrier, inc=1, device_id={"year": peer}, device_id_type=MESH)
-
     chunk_rows = rows // CHUNKS
 
     def chunk(index):
@@ -151,6 +143,14 @@
         load_losses(index).start()
     for index in (1, 6, 7, 8, 9, 10, 11):
         load(index).start()
+
+    barrier = pltpu.get_barrier_semaphore()
+    for step in range(1, n_port):
+        peer = lax.rem(me_port + step, n_port)
+        pl.semaphore_signal(barrier, inc=1, device_id={"port": peer}, device_id_type=MESH)
+    for step in range(1, n_year):
+        peer = lax.rem(me_year + step, n_year)
+        pl.semaphore_signal(barrier, inc=1, device_id={"year": peer}, device_id_type=MESH)
 
     def set_weights(dest, group):
         lane = lax.broadcasted_iota(jnp.int32, (LANES, ports), 0) + group * LANES
@@ -240,6 +240,7 @@
                 send_first(first_dest, first_device, 2)
             else:
                 send_piece(0, group, first_dest, first_device, 2)
+        for group in range(groups):
             send_piece(1, group, second_dest, second_dest, jnp.where(is_end, 1, 0))
             held[group] = product(last_dest, group)
 

time: 30.2 us -> 30.1 us (level)
  no operation moved by 1% of the time
where the time goes in v4:
time: 30.1 us; the launch traced here: 29.8 us
  Pallas kernels  29.2 us (97%)
  between operations  0.64 us (2%)
    pallas_call x1, Pallas kernels, on_device(): pl.pallas_call(functools.partial(kernel, sizes), name='layers', out_shape...  28.5 us
    pallas_call x1, Pallas kernels, on_device(): pl.pallas_call(put_out, name='put_out', out_shape=[jax.ShapeDtypeStruct(s...  0.66 us

profile of v4, /device:TPU:0, one launch (start us, length us, event | category | flops | bytes accessed | tf_op | source)
XLA Modules:
  0.0 29.8 jit_solution(10771445946318420765)
XLA Ops:
  0.6 28.5 %layers.1 = (f32[32,256]{1,0:T(8,128)S(1)}, f32[32,256]{1,0:T(8,128)S(1)}, f32[1,256]{1,0:T(1,128)S(1)}) custom-call(bf16[512,1024]{1,0:T(8,128)(2,1)} %refs_0_.1, s32[1,512]{1,0:T(1,128)} %bitcast.18, f32[1,1024]{1,0:T(1,128)} %bitcast.16, f32[1,1024]{1,0:T(1,128)} %bitcast.17, bf16[4,1024]{1,0:T(4,128)(2,1)} %bitcast.15, s32[4,1024]{1,0:T(4,128)} %bitcast.14, ...), custom_call_target="tpu_custom_call" | custom-call | tf_op jit(solution)/shard_map/layers/pallas_call | solution.py:410
  29.2 0.7 %put_out.1 = (f32[32,256]{1,0:T(8,128)}, f32[32,256]{1,0:T(8,128)}, f32[1,256]{1,0:T(1,128)}) custom-call(f32[32,256]{1,0:T(8,128)S(1)} %get-tuple-element.9.refs_0_, f32[32,256]{1,0:T(8,128)S(1)} %get-tuple-element.10.refs_1_, f32[1,256]{1,0:T(1,128)S(1)} %get-tuple-element.11.refs_2_), custom_call_target="tpu_custom_call" | custom-call | tf_op jit(solution)/shard_map/put_out/pallas_call | solution.py:434
